TPU v7x, 256 devices: a whole 4x4x8 slice. The times are simulated.
256 devices in a mesh: dp: 8 (over x, core), expert: 32 (over z, y).
Axes of the slice: x: 4, y: 4, z: 8, core: 2. Of those that a mesh axis runs over, the one named last changes fastest.
Arguments:
- tokens: bfloat16 [32768, 1024], P(('dp', 'expert')), may hold values from -6 to 6
- route_a: int32 [32768, 1], P(('dp', 'expert')), may hold values from 0 to 31
- route_b: int32 [32768, 1], P(('dp', 'expert')), may hold values from 0 to 63
- gain_a: float32 [1024], replicated, may hold values from 0.25 to 1.75
- gain_b: float32 [1024], replicated, may hold values from 0.25 to 1.75
- router_a: bfloat16 [1024, 32], replicated, may hold values from -0.375 to 0.375
- router_b: bfloat16 [1024, 64], replicated, may hold values from -0.375 to 0.375
- dense_in_a: bfloat16 [1024, 4096], P(None, 'dp'), may hold values from -0.1875 to 0.1875
- dense_out_a: bfloat16 [4096, 1024], P('dp'), may hold values from -0.09375 to 0.09375
- dense_in_b: bfloat16 [1024, 4096], P(None, 'dp'), may hold values from -0.1875 to 0.1875
- dense_out_b: bfloat16 [4096, 1024], P('dp'), may hold values from -0.09375 to 0.09375
- expert_in_a: bfloat16 [32, 1024, 4096], P('expert', None, 'dp'), may hold values from -0.1875 to 0.1875
- expert_out_a: bfloat16 [32, 4096, 1024], P('expert', 'dp'), may hold values from -0.09375 to 0.09375
- expert_in_b: bfloat16 [64, 1024, 4096], P('expert', None, 'dp'), may hold values from -0.1875 to 0.1875
- expert_out_b: bfloat16 [64, 4096, 1024], P('expert', 'dp'), may hold values from -0.09375 to 0.09375
Outputs:
- stream_out: bfloat16 [32768, 1024], P(('dp', 'expert'))
All inputs are finite; a program needn't handle non-finite values.
Results may differ from a plain program's by a relative error of at most 0.0091.
Values may be sent and summed in bfloat16 or wider, within the bound.
A program may use at most 128 MiB of HBM per device.

v0:
```python
import jax
import jax.numpy as jnp
from jax import lax
from jax.sharding import PartitionSpec as P


def in_order(blocks, dim):
    shape = list(blocks.shape[1:])
    shape[dim] *= blocks.shape[0]
    return jnp.moveaxis(blocks, 0, dim).reshape(shape)


def from_everyone(value, axis):
    copies = jnp.broadcast_to(value, (lax.axis_size(axis), *value.shape))
    return lax.all_to_all(copies, axis, split_axis=0, concat_axis=0, tiled=True)


def gather_directly(value, axis, dim):
    return in_order(from_everyone(value, axis), dim)


def in_blocks(value, dim, devices):
    before, after = (value.shape[:dim], value.shape[dim + 1 :])
    return jnp.moveaxis(value.reshape(*before, devices, -1, *after), dim, 0)


def summed_on_arrival(value, axis, dim):
    devices = lax.axis_size(axis)
    blocks = lax.all_to_all(in_blocks(value, dim, devices), axis, 0, 0, tiled=True)
    return jnp.sum(blocks.astype(jnp.float32), axis=0)


def norm_rows(x, gain):
    xf = x.astype(jnp.float32)
    mean = jnp.mean(xf, axis=-1, keepdims=True)
    var = jnp.mean((xf - mean) ** 2, axis=-1, keepdims=True)
    return ((xf - mean) / jnp.sqrt(var + 1e-05) * gain).astype(jnp.bfloat16)


def rank_table(blocks, experts):
    onehot = (blocks[:, :, None] == jnp.arange(experts)[None, None, :]).astype(jnp.int32)
    before = jnp.cumsum(onehot, axis=1) - onehot
    rank = jnp.sum(before * onehot, axis=-1)
    return (onehot, rank)


def moe_layer(x, ids, gain, router, d_in, d_out, e_in, e_out):
    tok_rows, width = x.shape
    experts = router.shape[1]
    owners = lax.axis_size("expert")
    per_dev = experts // owners
    cap = (5 * tok_rows + 4 * experts - 1) // (4 * experts)
    normed = norm_rows(x, gain)
    onehot, rank = rank_table(ids.reshape(1, tok_rows), experts)
    rank = rank.reshape(-1)
    kept = rank < cap
    total = experts * cap
    slot_row = jnp.where(kept, ids * cap + rank, total)
    logits = jnp.dot(normed, router, preferred_element_type=jnp.float32)
    picked = jnp.sum(logits * onehot.reshape(-1, experts).astype(jnp.float32), axis=-1)
    gate = jax.nn.sigmoid(picked) * kept.astype(jnp.float32)
    dense_act = jax.nn.gelu(
        jnp.dot(gather_directly(normed, "dp", 0), d_in, preferred_element_type=jnp.float32),
        approximate=True,
    ).astype(jnp.bfloat16)
    rows = dense_act
    dense = summed_on_arrival(
        jnp.dot(rows, d_out, preferred_element_type=jnp.float32).astype(jnp.bfloat16), "dp", 0
    )
    buffer = jnp.zeros((total, width), jnp.bfloat16).at[slot_row].set(normed, mode="drop")
    buffer = buffer.reshape(owners, per_dev, cap, width)
    arrived = lax.all_to_all(buffer, "expert", split_axis=0, concat_axis=0, tiled=True)
    expert_act = jax.nn.gelu(
        jnp.einsum(
            "secd,edf->secf",
            lax.all_gather(arrived, "dp", axis=0, tiled=True),
            e_in,
            preferred_element_type=jnp.float32,
        ),
        approximate=True,
    ).astype(jnp.bfloat16)
    rows = expert_act
    partial_value = lax.psum_scatter(
        jnp.einsum("secf,efd->secd", rows, e_out, preferred_element_type=jnp.float32).astype(
            jnp.bfloat16
        ),
        "dp",
        scatter_dimension=0,
        tiled=True,
    ).astype(jnp.float32)
    returned = (
        lax.all_to_all(
            partial_value.astype(jnp.bfloat16), "expert", split_axis=0, concat_axis=0, tiled=True
        )
        .astype(partial_value.dtype)
        .reshape(total, width)
    )
    expert_tok = jnp.take(returned, slot_row, axis=0, mode="fill", fill_value=0.0)
    return (x.astype(jnp.float32) + dense + gate[:, None] * expert_tok).astype(jnp.bfloat16)


def body(
    tokens,
    route_a,
    route_b,
    gain_a,
    gain_b,
    router_a,
    router_b,
    dense_in_a,
    dense_out_a,
    dense_in_b,
    dense_out_b,
    expert_in_a,
    expert_out_a,
    expert_in_b,
    expert_out_b,
):
    middle = moe_layer(
        tokens, route_a[:, 0], gain_a, router_a, dense_in_a, dense_out_a, expert_in_a, expert_out_a
    )
    return moe_layer(
        middle, route_b[:, 0], gain_b, router_b, dense_in_b, dense_out_b, expert_in_b, expert_out_b
    )


def solution(mesh):
    in_specs = (
        P(("dp", "expert"), None),
        P(("dp", "expert"), None),
        P(("dp", "expert"), None),
        P(),
        P(),
        P(),
        P(),
        P(None, "dp"),
        P("dp", None),
        P(None, "dp"),
        P("dp", None),
        P("expert", None, "dp"),
        P("expert", "dp", None),
        P("expert", None, "dp"),
        P("expert", "dp", None),
    )
    out_specs = P(("dp", "expert"), None)
    return jax.shard_map(body, mesh=mesh, in_specs=in_specs, out_specs=out_specs, check_vma=False)
```

profile of v0, /device:TPU:32, one launch (start us, length us, event | category | flops | bytes accessed | tf_op | source)
XLA Modules:
  0.0 354.0 jit_solution(15019719602853124694)
XLA Ops:
  6.5 0.9 fusion.83
  7.4 0.2 reduce_window_sum.22
  7.6 0.8 select_reduce_fusion.1
  8.4 0.7 and_bitcast_fusion.1
  9.1 1.1 convert_reduce_fusion.3
  10.2 1.2 fusion.71
  11.4 1.8 scatter_custom_fusion
  13.1 0.1 reshape.321
  13.3 28.4 %all_to_all.40 = bf16[32,1,5,1024]{3,2,1,0:T(8,128)(2,1)S(1)} all-to-all(bf16[32,1,5,1024]{3,2,1,0:T(8,128)(2,1)S(1)} %bitcast.99), channel_id=1, replica_groups=mesh['dp'=8,'expert'=32] {'expert'}, dimensions={0} | all-to-all | bytes 655360 | tf_op jit(solution)/shard_map/all_to_all | solution.py:72
  41.6 0.9 copy.33
  42.6 0.0 all-gather.3.cloned.1.call-update
  42.6 0.0 reduce-scatter.3.cloned.1.call-start
  42.6 25.1 %all-gather.3.cloned.1.call-done = bf16[256,1,5,1024]{3,0,2,1:T(8,128)(2,1)} async-done(((bf16[32,1,5,1024]{3,0,2,1:T(8,128)(2,1)}), bf16[256,1,5,1024]{3,0,2,1:T(8,128)(2,1)}) %all-gather.3.cloned.1.call-update) | async-done | bytes 2621456 | tf_op jit(solution)/shard_map/all_gather | solution.py:76
  67.7 7.1 %convert_bitcast_fusion.1 = bf16[256,1,5,1024]{3,0,2,1:T(8,128)(2,1)} fusion(bf16[1,512,1024]{2,1,0:T(8,128)(2,1)} %param.27, bf16[256,1,5,1024]{3,0,2,1:T(8,128)(2,1)} %all-gather.3.cloned.1.call-done, bf16[1,1024,512]{2,1,0:T(8,128)(2,1)} %param.26), kind=kOutput, calls=%fused_computation.29 | convolution fusion | flops 2691563520 | bytes 7340032 | tf_op jit(solution)/shard_map/secf,efd->secd/dot_general | solution.py:84
  74.9 0.0 reduce-scatter.3.cloned.1.call-update
  74.9 0.9 copy-done.1
  75.8 0.2 fusion.73
  76.0 0.3 broadcast_in_dim.49
  76.2 39.3 %all_to_all.41 = bf16[8,128,1024]{2,1,0:T(8,128)(2,1)} all-to-all(bf16[8,128,1024]{2,1,0:T(8,128)(2,1)S(1)} %broadcast_in_dim.49), channel_id=1, replica_groups=mesh['dp'=8,'expert'=32] {'dp'}, dimensions={0} | all-to-all | bytes 4194304 | tf_op jit(solution)/shard_map/all_to_all | solution.py:15
  115.5 6.2 %convolution_convert_fusion.1 = bf16[1024,1024]{1,0:T(8,128)(2,1)} fusion(bf16[512,1024]{1,0:T(8,128)(2,1)} %param.23, bf16[1024,1024]{1,0:T(8,128)(2,1)} %bitcast.97, bf16[1024,512]{1,0:T(8,128)(2,1)} %param.22), kind=kOutput, calls=%fused_computation.50 | convolution fusion | flops 2153250816 | bytes 6291456 | tf_op jit(solution)/shard_map/dot_general | solution.py:68
  121.7 4.5 %all-to-all-start.1 = ((bf16[8,128,1024]{2,1,0:T(8,128)(2,1)}), bf16[8,128,1024]{2,1,0:T(8,128)(2,1)}, u32[]{:S(2)}, u32[]{:S(2)}) async-start(bf16[8,128,1024]{2,1,0:T(8,128)(2,1)} %bitcast.95), calls=%async_computation.1 | async-start | bytes 4194304 | tf_op jit(solution)/shard_map/all_to_all | solution.py:29
  126.2 0.1 fusion.82
  126.3 0.2 reduce_window_sum.23
  126.5 0.2 select_reduce_fusion
  126.7 0.2 fusion.45
  126.9 0.0 reduce-scatter.3.cloned.1.call-done
  126.9 2.0 copy.34
  128.9 24.5 %all-to-all-done.1 = bf16[8,128,1024]{2,1,0:T(8,128)(2,1)} async-done(((bf16[8,128,1024]{2,1,0:T(8,128)(2,1)}), bf16[8,128,1024]{2,1,0:T(8,128)(2,1)}, u32[]{:S(2)}, u32[]{:S(2)}) %all-to-all-start.1) | async-done | bytes 2097184 | tf_op jit(solution)/shard_map/all_to_all | solution.py:29
  153.4 10.1 %all-to-all-start.3 = ((bf16[32,1,5,1024]{3,2,1,0:T(8,128)(2,1)}), bf16[32,1,5,1024]{3,2,1,0:T(8,128)(2,1)}, u32[]{:S(2)}, u32[]{:S(2)}) async-start(bf16[32,1,5,1024]{3,2,1,0:T(8,128)(2,1)} %copy.34), calls=%async_computation.4 | async-start | bytes 1048576 | tf_op jit(solution)/shard_map/all_to_all | solution.py:92
  163.5 0.0 all-gather.5.cloned.1.call-start
  163.6 2.8 convert_reduce_fusion.1
  166.4 14.1 %all-to-all-done.3 = bf16[32,1,5,1024]{3,2,1,0:T(8,128)(2,1)} async-done(((bf16[32,1,5,1024]{3,2,1,0:T(8,128)(2,1)}), bf16[32,1,5,1024]{3,2,1,0:T(8,128)(2,1)}, u32[]{:S(2)}, u32[]{:S(2)}) %all-to-all-start.3) | async-done | bytes 327712 | tf_op jit(solution)/shard_map/all_to_all | solution.py:92
  180.5 1.2 reshape.334
  181.6 0.0 copy-start.5
  181.7 1.6 gather_fusion
  183.2 1.4 convert_reduce_fusion.2
  184.7 0.2 fusion.68
  184.9 1.4 scatter_custom_fusion.1
  186.3 0.2 reshape.330
  186.5 0.3 copy.35
  186.9 18.9 %all_to_all.42 = bf16[32,2,3,1024]{3,1,2,0:T(2,128)(2,1)S(1)} all-to-all(bf16[32,2,3,1024]{3,1,2,0:T(2,128)(2,1)S(1)} %copy.35), channel_id=1, replica_groups=mesh['dp'=8,'expert'=32] {'expert'}, dimensions={0} | all-to-all | bytes 786432 | tf_op jit(solution)/shard_map/all_to_all | solution.py:72
  205.7 0.8 copy.36
  206.6 0.0 all-gather.5.cloned.1.call-update
  206.6 0.2 reduce-scatter.5.cloned.1.call-start
  206.8 24.4 %all-gather.5.cloned.1.call-done = bf16[256,2,3,1024]{3,0,2,1:T(8,128)(2,1)} async-done(((bf16[32,2,3,1024]{3,0,2,1:T(8,128)(2,1)}), bf16[256,2,3,1024]{3,0,2,1:T(8,128)(2,1)}) %all-gather.5.cloned.1.call-update) | async-done | bytes 3145744 | tf_op jit(solution)/shard_map/all_gather | solution.py:76
  231.2 7.9 %convert_bitcast_fusion = bf16[256,2,3,1024]{3,0,2,1:T(8,128)(2,1)} fusion(bf16[2,512,1024]{2,1,0:T(8,128)(2,1)S(1)} %copy-done, bf16[256,2,3,1024]{3,0,2,1:T(8,128)(2,1)} %all-gather.5.cloned.1.call-done, bf16[2,1024,512]{2,1,0:T(8,128)(2,1)} %param.28), kind=kOutput, calls=%fused_computation.16 | convolution fusion | flops 3229876224 | bytes 10485760 | tf_op jit(solution)/shard_map/secf,efd->secd/dot_general | solution.py:84
  239.1 0.0 reduce-scatter.5.cloned.1.call-update
  239.1 0.2 fusion.70
  239.3 0.3 broadcast_in_dim.54
  239.5 38.7 %all_to_all.43 = bf16[8,128,1024]{2,1,0:T(8,128)(2,1)} all-to-all(bf16[8,128,1024]{2,1,0:T(8,128)(2,1)S(1)} %broadcast_in_dim.54), channel_id=1, replica_groups=mesh['dp'=8,'expert'=32] {'dp'}, dimensions={0} | all-to-all | bytes 4194304 | tf_op jit(solution)/shard_map/all_to_all | solution.py:15
  278.3 6.2 %convolution_convert_fusion = bf16[1024,1024]{1,0:T(8,128)(2,1)} fusion(bf16[512,1024]{1,0:T(8,128)(2,1)} %param.25, bf16[1024,1024]{1,0:T(8,128)(2,1)} %bitcast.98, bf16[1024,512]{1,0:T(8,128)(2,1)} %param.24), kind=kOutput, calls=%fused_computation.49 | convolution fusion | flops 2153250816 | bytes 6291456 | tf_op jit(solution)/shard_map/dot_general | solution.py:68
  284.5 4.5 %all-to-all-start.5 = ((bf16[8,128,1024]{2,1,0:T(8,128)(2,1)}), bf16[8,128,1024]{2,1,0:T(8,128)(2,1)}, u32[]{:S(2)}, u32[]{:S(2)}) async-start(bf16[8,128,1024]{2,1,0:T(8,128)(2,1)} %bitcast.96), calls=%async_computation.6 | async-start | bytes 4194304 | tf_op jit(solution)/shard_map/all_to_all | solution.py:29
  289.0 0.9 reduce-scatter.5.cloned.1.call-done
  289.9 2.1 copy.37
  292.0 24.2 %all-to-all-done.5 = bf16[8,128,1024]{2,1,0:T(8,128)(2,1)} async-done(((bf16[8,128,1024]{2,1,0:T(8,128)(2,1)}), bf16[8,128,1024]{2,1,0:T(8,128)(2,1)}, u32[]{:S(2)}, u32[]{:S(2)}) %all-to-all-start.5) | async-done | bytes 2097184 | tf_op jit(solution)/shard_map/all_to_all | solution.py:29
  316.1 10.1 %all-to-all-start.7 = ((bf16[32,2,3,1024]{3,1,2,0:T(2,128)(2,1)}), bf16[32,2,3,1024]{3,1,2,0:T(2,128)(2,1)S(1)}, u32[]{:S(2)}, u32[]{:S(2)}) async-start(bf16[32,2,3,1024]{3,1,2,0:T(2,128)(2,1)} %copy.37), calls=%async_computation.9 | async-start | bytes 786432 | tf_op jit(solution)/shard_map/all_to_all | solution.py:92
  326.3 0.2 fusion.44
  326.5 2.8 convert_reduce_fusion
  329.3 11.3 %all-to-all-done.7 = bf16[32,2,3,1024]{3,1,2,0:T(2,128)(2,1)S(1)} async-done(((bf16[32,2,3,1024]{3,1,2,0:T(2,128)(2,1)}), bf16[32,2,3,1024]{3,1,2,0:T(2,128)(2,1)S(1)}, u32[]{:S(2)}, u32[]{:S(2)}) %all-to-all-start.7) | async-done | bytes 393248 | tf_op jit(solution)/shard_map/all_to_all | solution.py:92
  340.6 0.1 copy_convert_fusion
  340.7 1.5 copy.39
  342.3 1.6 reshape.336
  343.9 1.6 gather_fusion.1
  345.4 2.0 fusion.77
  (24 shorter events, 0.1 us)
Async XLA Ops:
  6.5 224.7 %copy-start = (bf16[2,512,1024]{2,1,0:T(8,128)(2,1)S(1)}, bf16[2,512,1024]{2,1,0:T(8,128)(2,1)}, u32[]{:S(2)}) copy-start(bf16[2,512,1024]{2,1,0:T(8,128)(2,1)} %param.29) | copy-start | bytes 6291460
  6.5 61.2 %all-gather.3.cloned.1.call-start = ((), (), s32[]{:S(2)}) async-start(), calls=%async_computation.10 | async-start | bytes 2949120 | tf_op jit(solution)/shard_map/all_gather | solution.py:76
  42.6 84.3 %reduce-scatter.3.cloned.1.call-start = ((), (), s32[]{:S(2)}) async-start(), calls=%async_computation.11 | async-start | bytes 2949120 | tf_op jit(solution)/shard_map/reduce_scatter | solution.py:83
  74.9 0.9 copy-start.1
  74.9 1.0 copy-start.4
  121.7 4.5 %copy-start.7 = (s32[128,1]{0,1:T(1,128)S(1)}, s32[128,1]{0,1:T(1,128)}, u32[]{:S(2)}) copy-start(s32[128,1]{0,1:T(1,128)} %param.17) | copy-start | bytes 1540
  121.7 5.0 %copy-start.3 = (bf16[1024,32]{0,1:T(8,128)(2,1)S(1)}, bf16[1024,32]{0,1:T(8,128)(2,1)}, u32[]{:S(2)}) copy-start(bf16[1024,32]{0,1:T(8,128)(2,1)} %param.20) | copy-start | bytes 196612
  121.7 5.0 %copy-start.6 = (s32[128,1]{0,1:T(1,128)S(1)}, s32[128,1]{0,1:T(1,128)}, u32[]{:S(2)}) copy-start(s32[128,1]{0,1:T(1,128)} %param.16) | copy-start | bytes 1540
  121.7 31.7 %all-to-all-start.1 = ((bf16[8,128,1024]{2,1,0:T(8,128)(2,1)}), bf16[8,128,1024]{2,1,0:T(8,128)(2,1)}, u32[]{:S(2)}, u32[]{:S(2)}) async-start(bf16[8,128,1024]{2,1,0:T(8,128)(2,1)} %bitcast.95), calls=%async_computation.1 | async-start | bytes 4194304 | tf_op jit(solution)/shard_map/all_to_all | solution.py:29
  153.4 27.1 %all-to-all-start.3 = ((bf16[32,1,5,1024]{3,2,1,0:T(8,128)(2,1)}), bf16[32,1,5,1024]{3,2,1,0:T(8,128)(2,1)}, u32[]{:S(2)}, u32[]{:S(2)}) async-start(bf16[32,1,5,1024]{3,2,1,0:T(8,128)(2,1)} %copy.34), calls=%async_computation.4 | async-start | bytes 1048576 | tf_op jit(solution)/shard_map/all_to_all | solution.py:92
  163.5 67.7 %all-gather.5.cloned.1.call-start = ((), (), s32[]{:S(2)}) async-start(), calls=%async_computation.12 | async-start | bytes 3538944 | tf_op jit(solution)/shard_map/all_gather | solution.py:76
  181.6 3.3 copy-start.5
  206.6 83.3 %reduce-scatter.5.cloned.1.call-start = ((), (), s32[]{:S(2)}) async-start(), calls=%async_computation.13 | async-start | bytes 3538944 | tf_op jit(solution)/shard_map/reduce_scatter | solution.py:83
  284.5 41.8 %copy-start.2 = (bf16[1024,64]{0,1:T(8,128)(2,1)S(1)}, bf16[1024,64]{0,1:T(8,128)(2,1)}, u32[]{:S(2)}) copy-start(bf16[1024,64]{0,1:T(8,128)(2,1)} %param.21) | copy-start | bytes 393220
  284.5 31.7 %all-to-all-start.5 = ((bf16[8,128,1024]{2,1,0:T(8,128)(2,1)}), bf16[8,128,1024]{2,1,0:T(8,128)(2,1)}, u32[]{:S(2)}, u32[]{:S(2)}) async-start(bf16[8,128,1024]{2,1,0:T(8,128)(2,1)} %bitcast.96), calls=%async_computation.6 | async-start | bytes 4194304 | tf_op jit(solution)/shard_map/all_to_all | solution.py:29
  316.1 24.5 %all-to-all-start.7 = ((bf16[32,2,3,1024]{3,1,2,0:T(2,128)(2,1)}), bf16[32,2,3,1024]{3,1,2,0:T(2,128)(2,1)S(1)}, u32[]{:S(2)}, u32[]{:S(2)}) async-start(bf16[32,2,3,1024]{3,1,2,0:T(2,128)(2,1)} %copy.37), calls=%async_computation.9 | async-start | bytes 786432 | tf_op jit(solution)/shard_map/all_to_all | solution.py:92
Sparse Core Ops, SparseCore 0:
  42.7 24.9 all-gather.2
  75.0 49.9 reduce-scatter.2
  206.7 24.4 all-gather.4
  239.2 50.5 reduce-scatter.4
where the time goes:
time: 355 us; the launch traced here: 354 us
  blocking collectives  125 us (35%)
  waiting for transfers between devices  124 us (35%)
  starting transfers between devices  29.5 us (8%)
  matrix products  27.8 us (8%)
  other arithmetic  18.2 us (5%)
  local copies, waits for them, and re-layouts  15.4 us (4%)
  between operations  13.4 us (4%)
    all_to_all x2, blocking collectives, from_everyone(): return lax.all_to_all(copies, axis, split_axis=0, concat_axis=0, tiled=True)  78 us
    all_gather x2, waiting for transfers between devices, moe_layer(): lax.all_gather(arrived, 'dp', axis=0, tiled=True)  49.5 us
    all_to_all x2, waiting for transfers between devices, summed_on_arrival(): lax.all_to_all(in_blocks(value, dim, devices), axis, 0, 0, tiled=True)  48.7 us
    all_to_all x2, blocking collectives, moe_layer(): lax.all_to_all(buffer, 'expert', split_axis=0, concat_axis=0, tiled=True)  47.2 us
    all_to_all x2, waiting for transfers between devices, moe_layer(): lax.all_to_all(partial_value.astype(jnp.bfloat16), 'expert', split_axis=0...  25.4 us
    all_to_all x2, starting transfers between devices, moe_layer(): lax.all_to_all(partial_value.astype(jnp.bfloat16), 'expert', split_axis=0...  20.2 us
    dot_general x2, matrix products, moe_layer(): jnp.einsum('secf,efd->secd', rows, e_out, preferred_element_type=jnp.floa...  15 us
    dot_general x2, matrix products, moe_layer(): jnp.dot(rows, d_out, preferred_element_type=jnp.float32)  12.4 us
  transfers between devices with their start and end apart: 8, of which 7 were waited for; matrix products, arithmetic and copies ran while one was open for 7% of the time, Pallas kernels for 0%

commit v1 on v0

v1 whole, which is shorter than its diff:
```python
import functools

import jax
import jax.numpy as jnp
from jax import lax
from jax.experimental import pallas as pl
from jax.experimental.pallas import tpu as pltpu
from jax.sharding import PartitionSpec as P

MESH = pl.DeviceIdType.MESH
BF = jnp.bfloat16
F32 = jnp.float32
PAD = 8


def dot(a, b):
    return jnp.dot(a, b, preferred_element_type=F32)


def ffn(rows, w_in, w_out):
    return dot(jax.nn.gelu(dot(rows, w_in), approximate=True).astype(BF), w_out)


class Place:
    def __init__(self, n_dp, n_ex):
        self.n_ex = n_ex
        chips = n_dp // 2
        self.d = lax.axis_index("dp")
        self.e = lax.axis_index("expert")
        x, c = self.d // 2, self.d % 2
        right = (lax.rem(x + 1, chips) * 2 + c, self.e)
        left = (lax.rem(x + chips - 1, chips) * 2 + c, self.e)
        self.along = (right, left)
        self.partner = (x * 2 + 1 - c, self.e)

    def ahead(self, o):
        return (self.d, lax.rem(self.e + o, self.n_ex))

    def behind(self, o):
        return (self.d, lax.rem(self.e + self.n_ex - o, self.n_ex))


class Ring:
    def __init__(self, place, blocks, partial, kept, sums, landed, sems):
        self.p = place
        self.g = blocks
        self.y1 = partial
        self.y0 = kept
        self.s = sums
        self.z = landed[0]
        self.f = landed[1]
        self.link_send, self.link_recv, self.core_send, self.core_recv = sems
        self.started = []

    def copy(self, src, dst, kind, slot, to):
        send, recv = (self.link_send, self.link_recv) if kind else (self.core_send, self.core_recv)
        return pltpu.make_async_remote_copy(
            src_ref=src,
            dst_ref=dst,
            send_sem=send.at[slot],
            recv_sem=recv.at[slot],
            device_id=to,
            device_id_type=MESH,
        )

    def start(self, make):
        made = make
        made.start()
        self.started.append(made)

    def gather_copy(self, u, h):
        if u == 1:
            return self.copy(self.g.at[0, h, 0], self.g.at[1, h, 0], 1, h, self.p.along[h])
        if u == 2:
            return self.copy(self.g.at[0, h, 0], self.g.at[2, h, 0], 1, 2 + h, self.p.along[1 - h])
        return self.copy(self.g.at[1, h, 0], self.g.at[3, h, 0], 1, 4 + h, self.p.along[h])

    def core_copy(self, u, h):
        return self.copy(self.g.at[u, h, 0], self.g.at[u, h, 1], 0, 2 * u + h, self.p.partner)

    def gather_start(self):
        for u in (1, 2):
            for h in (0, 1):
                self.start(self.gather_copy(u, h))
        for h in (0, 1):
            self.start(self.core_copy(0, h))

    def arrive(self, u):
        for h in (0, 1):
            self.gather_copy(u, h).wait_recv()
            if u == 1:
                self.start(self.gather_copy(3, h))
            self.start(self.core_copy(u, h))

    def compute(self, u, fn):
        for h in (0, 1):
            self.core_copy(u, h).wait_recv()
        fn(u)
        for h in (0, 1):
            self.start(self.sum_copy(u, h))

    def sum_copy(self, u, h):
        return self.copy(self.y1.at[u, h], self.z.at[u, h], 0, 8 + 2 * u + h, self.p.partner)

    def core_sum(self, u, h):
        self.sum_copy(u, h).wait_recv()
        return self.y0[u, h] + self.z[u, h].astype(F32)

    def scatter_copy(self, u, h):
        to = self.p.along[1 - h] if u == 1 else self.p.along[h]
        slot = {1: 0, 3: 1, 2: 2}[u]
        return self.copy(self.s.at[slot, h], self.f.at[slot, h], 1, 6 + 2 * slot + h, to)

    def scatter_near(self):
        for h in (0, 1):
            self.s[0, h] = self.core_sum(1, h).astype(BF)
            self.start(self.scatter_copy(1, h))

    def scatter_far(self):
        for h in (0, 1):
            self.s[1, h] = self.core_sum(3, h).astype(BF)
            self.start(self.scatter_copy(3, h))

    def scatter_last(self):
        for h in (0, 1):
            mine = self.core_sum(2, h)
            self.scatter_copy(3, h).wait_recv()
            self.s[2, h] = (mine + self.f[1, h].astype(F32)).astype(BF)
            self.start(self.scatter_copy(2, h))

    def total(self, h):
        mine = self.core_sum(0, h)
        self.scatter_copy(1, h).wait_recv()
        mine = mine + self.f[0, h].astype(F32)
        self.scatter_copy(2, h).wait_recv()
        return mine + self.f[2, h].astype(F32)

    def drain(self):
        for made in self.started:
            made.wait_send()


class Exchange:
    def __init__(self, place, out, into, send, recv, forward):
        self.p, self.out, self.into, self.send, self.recv = place, out, into, send, recv
        self.forward = forward

    def copy(self, o):
        return pltpu.make_async_remote_copy(
            src_ref=self.out.at[o],
            dst_ref=self.into.at[o],
            send_sem=self.send.at[o],
            recv_sem=self.recv.at[o],
            device_id=self.p.ahead(o) if self.forward else self.p.behind(o),
            device_id_type=MESH,
        )

    def start(self):
        def one(o, carry):
            self.copy(o).start()
            return carry

        lax.fori_loop(1, self.p.n_ex, one, 0)

    def arrived(self):
        def one(o, carry):
            self.copy(o).wait_recv()
            return carry

        lax.fori_loop(1, self.p.n_ex, one, 0)

    def drain(self):
        def one(o, carry):
            self.copy(o).wait_send()
            return carry

        lax.fori_loop(1, self.p.n_ex, one, 0)


def norm_rows(xf, gain):
    mean = jnp.mean(xf, axis=-1, keepdims=True)
    var = jnp.mean((xf - mean) ** 2, axis=-1, keepdims=True)
    return ((xf - mean) / jnp.sqrt(var + 1e-05) * gain).astype(BF)


def iota(shape, dim):
    return lax.broadcasted_iota(jnp.int32, shape, dim)


def routing(ids, place, experts, cap):
    tok = ids.shape[0]
    per_dev = experts // place.n_ex
    onehot = (ids == iota((tok, experts), 1)).astype(F32)
    below = (iota((tok, tok), 1) < iota((tok, tok), 0)).astype(F32)
    before = dot(below.astype(BF), onehot.astype(BF))
    rank = jnp.sum(before * onehot, axis=-1, keepdims=True)
    kept = rank < cap
    owner, inner = ids // per_dev, ids % per_dev
    offset = lax.rem(owner - place.e + place.n_ex, place.n_ex)
    row = (offset * PAD + inner * cap).astype(F32) + rank
    rows = place.n_ex * PAD
    spot = jnp.where(kept & (iota((tok, rows), 1).astype(F32) == row), 1.0, 0.0)
    return onehot, kept, spot


def packed_row(p, place, per_dev, cap):
    source, inner = p // PAD, p % PAD
    row = inner
    which = jnp.zeros_like(p)
    for k in range(1, per_dev):
        which = which + (inner >= k * cap).astype(jnp.int32)
    row = inner - which * cap
    return jnp.where(
        inner < per_dev * cap, which * (place.n_ex * cap) + source * cap + row, -1
    )


def kernel(
    n_dp,
    n_ex,
    *refs,
):
    (tokens, route_a, route_b, gain_a, gain_b, router_a, router_b) = refs[:7]
    weights = refs[7:15]
    out = refs[15]
    local = refs[16:24]
    weight_sem = refs[24]
    scratch = refs[25:]
    place = Place(n_dp, n_ex)
    loads = [
        pltpu.make_async_copy(weights[i], local[i], weight_sem.at[i]) for i in range(8)
    ]
    barrier = pltpu.get_barrier_semaphore()

    def greet(o, carry):
        pl.semaphore_signal(barrier, inc=1, device_id=place.ahead(o), device_id_type=MESH)
        return carry

    for to in (*place.along, place.partner):
        pl.semaphore_signal(barrier, inc=1, device_id=to, device_id_type=MESH)
    lax.fori_loop(1, n_ex, greet, 0)
    for i in (0, 1, 4, 5, 2, 3, 6, 7):
        loads[i].start()

    kept_dense, kept_expert = scratch[:2]
    per_layer = (len(scratch) - 2) // 2
    drains = []
    x = tokens[...].astype(F32)
    for layer in range(2):
        s = scratch[2 + layer * per_layer : 2 + (layer + 1) * per_layer]
        dense = Ring(place, s[0], s[1], kept_dense, s[2], s[3:5], s[5:9])
        s = s[9:]
        rows = s[0].shape[3]
        y0 = kept_expert.at[:, :, pl.ds(0, rows)]
        expert = Ring(place, s[0], s[1], y0, s[2], s[3:5], s[5:9])
        s = s[9:]
        go = Exchange(place, s[0], s[1], s[2], s[3], True)
        back = Exchange(place, s[4], s[5], s[6], s[7], False)
        drains += [dense, expert, go, back]
        ids = (route_a, route_b)[layer][...]
        router = (router_a, router_b)[layer][...]
        experts = router.shape[1]
        tok, width = tokens.shape
        per_dev = experts // n_ex
        cap = (5 * tok + 4 * experts - 1) // (4 * experts)
        d_in, d_out = local[4 * layer], local[4 * layer + 1]
        e_in, e_out = local[4 * layer + 2], local[4 * layer + 3]
        half = tok // 2

        normed = norm_rows(x, (gain_a, gain_b)[layer][...])
        for h in (0, 1):
            dense.g[0, h, 0] = normed[h * half : (h + 1) * half]
        onehot, kept, spot = routing(ids, place, experts, cap)
        if layer == 0:
            pl.semaphore_wait(barrier, n_ex - 1 + 3)
        dense.gather_start()
        messages = dot(spot.T.astype(BF), normed).astype(BF).reshape(n_ex, PAD, width)
        go.out[...] = messages
        go.into[0] = messages[0]
        go.start()
        logits = dot(normed, router)
        picked = jnp.sum(logits * onehot, axis=-1, keepdims=True)
        gate = jax.nn.sigmoid(picked) * kept.astype(F32)

        def dense_unit(u):
            y = ffn(dense.g[u].reshape(4 * half, width), d_in[...], d_out[...])
            y = y.reshape(2, 2, half, width)
            dense.y1[u] = y[:, 1].astype(BF)
            dense.y0[u] = y[:, 0]

        def expert_unit(u):
            if per_dev == 1:
                y = ffn(expert.g[u].reshape(4 * rows, width), e_in[0], e_out[0])
                y = y.reshape(2, 2, rows, width)
                expert.y1[u] = y[:, 1].astype(BF)
                expert.y0[u] = y[:, 0]
            else:
                for h in (0, 1):
                    y = ffn(expert.g[u, h].reshape(2 * rows, width), e_in[h], e_out[h])
                    y = y.reshape(2, rows, width)
                    expert.y1[u, h] = y[1].astype(BF)
                    expert.y0[u, h] = y[0]

        for i in (0, 1):
            loads[4 * layer + i].wait()
        dense.compute(0, dense_unit)
        dense.arrive(1)
        dense.compute(1, dense_unit)
        dense.arrive(2)

        go.arrived()
        slots = n_ex * PAD
        message = iota((2 * rows, slots), 1)
        pack = packed_row(message, place, per_dev, cap) == iota((2 * rows, slots), 0)
        block = dot(
            jnp.where(pack, 1.0, 0.0).astype(BF), go.into[...].reshape(slots, width)
        ).astype(BF)
        for h in (0, 1):
            expert.g[0, h, 0] = block[h * rows : (h + 1) * rows]
        expert.gather_start()
        dense.compute(2, dense_unit)
        dense.arrive(3)
        dense.compute(3, dense_unit)
        for i in (2, 3):
            loads[4 * layer + i].wait()
        expert.compute(0, expert_unit)
        expert.arrive(1)
        expert.compute(1, expert_unit)
        expert.arrive(2)
        expert.compute(2, expert_unit)
        expert.scatter_near()
        expert.arrive(3)
        expert.compute(3, expert_unit)
        expert.scatter_far()
        dense.scatter_near()
        expert.scatter_last()
        dense.scatter_far()
        block = jnp.concatenate([expert.total(h) for h in (0, 1)], axis=0).astype(BF)
        message = iota((slots, 2 * rows), 0)
        unpack = packed_row(message, place, per_dev, cap) == iota((slots, 2 * rows), 1)
        messages = (
            dot(jnp.where(unpack, 1.0, 0.0).astype(BF), block)
            .astype(BF)
            .reshape(n_ex, PAD, width)
        )
        back.out[...] = messages
        back.into[0] = messages[0]
        back.start()
        dense.scatter_last()
        summed = jnp.concatenate([dense.total(h) for h in (0, 1)], axis=0)
        back.arrived()
        found = dot(spot.astype(BF), back.into[...].reshape(slots, width))
        result = (x + summed + gate * found).astype(BF)
        x = result.astype(F32)
    out[...] = result
    for thing in drains:
        thing.drain()


def ring_scratch(rows, width):
    block = lambda *lead: pltpu.VMEM((*lead, rows, width), BF)
    return [
        block(4, 2, 2),
        block(4, 2),
        block(3, 2),
        block(4, 2),
        block(3, 2),
        pltpu.SemaphoreType.DMA((12,)),
        pltpu.SemaphoreType.DMA((12,)),
        pltpu.SemaphoreType.DMA((16,)),
        pltpu.SemaphoreType.DMA((16,)),
    ]


def exchange_scratch(n_ex, width):
    one = pltpu.VMEM((n_ex, PAD, width), BF)
    sem = pltpu.SemaphoreType.DMA((n_ex,))
    return [one, one, sem, sem]


def body(n_dp, n_ex, *args):
    tokens, route_a, route_b, gain_a, gain_b, router_a, router_b = args[:7]
    dense_in_a, dense_out_a, dense_in_b, dense_out_b = args[7:11]
    expert_in_a, expert_out_a, expert_in_b, expert_out_b = args[11:15]
    weights = (
        dense_in_a,
        dense_out_a,
        expert_in_a,
        expert_out_a,
        dense_in_b,
        dense_out_b,
        expert_in_b,
        expert_out_b,
    )
    tok, width = tokens.shape
    scratch = [pltpu.VMEM(w.shape, BF) for w in weights]
    scratch.append(pltpu.SemaphoreType.DMA((8,)))
    per_half = []
    layers = []
    for router in (router_a, router_b):
        experts = router.shape[1]
        cap = (5 * tok + 4 * experts - 1) // (4 * experts)
        rows = experts * cap // 2
        per_half.append(rows)
        layers += ring_scratch(tok // 2, width) + ring_scratch(rows, width)
        layers += exchange_scratch(n_ex, width) * 2
    scratch.append(pltpu.VMEM((4, 2, tok // 2, width), F32))
    scratch.append(pltpu.VMEM((4, 2, max(per_half), width), F32))
    scratch += layers
    vmem = pl.BlockSpec(memory_space=pltpu.VMEM)
    return pl.pallas_call(
        functools.partial(kernel, n_dp, n_ex),
        out_shape=jax.ShapeDtypeStruct((tok, width), BF),
        in_specs=[vmem] * 7 + [pl.BlockSpec(memory_space=pl.ANY)] * 8,
        out_specs=vmem,
        scratch_shapes=scratch,
        compiler_params=pltpu.CompilerParams(
            collective_id=0, has_side_effects=True, vmem_limit_bytes=67043328
        ),
    )(
        tokens,
        route_a,
        route_b,
        gain_a.reshape(1, width),
        gain_b.reshape(1, width),
        router_a,
        router_b,
        *weights,
    )


def solution(mesh):
    in_specs = (
        P(("dp", "expert"), None),
        P(("dp", "expert"), None),
        P(("dp", "expert"), None),
        P(),
        P(),
        P(),
        P(),
        P(None, "dp"),
        P("dp", None),
        P(None, "dp"),
        P("dp", None),
        P("expert", None, "dp"),
        P("expert", "dp", None),
        P("expert", None, "dp"),
        P("expert", "dp", None),
    )
    out_specs = P(("dp", "expert"), None)
    return jax.shard_map(
        functools.partial(body, mesh.shape["dp"], mesh.shape["expert"]),
        mesh=mesh,
        in_specs=in_specs,
        out_specs=out_specs,
        check_vma=False,
    )
```

time: 355 us -> 149 us (0.42)
  Pallas kernels: 0 us -> 139 us
  blocking collectives: 125 us -> 0 us
  waiting for transfers between devices: 124 us -> 0 us
  starting transfers between devices: 29.5 us -> 0 us
  matrix products: 27.8 us -> 0 us
  other arithmetic: 18.2 us -> 0 us
  between operations: 13.4 us -> 0.01 us
  local copies, waits for them, and re-layouts: 15.4 us -> 7.84 us
    pallas_call x0 -> x1, Pallas kernels: none -> 139 us  [body(): pl.pallas_call(functools.partial(kernel, n_dp, n_ex), out_shape=jax.Shape...]
    all_to_all x4 -> x0, blocking collectives: 125 us -> none  [the longest x2 78 us: from_everyone(): return lax.all_to_all(copies, axis, split_axis=0, concat_axis=0, tiled=True)]
    all_to_all x4 -> x0, waiting for transfers between devices: 74.1 us -> none  [the longest x2 48.7 us: summed_on_arrival(): lax.all_to_all(in_blocks(value, dim, devices), axis, 0, 0, tiled=True)]
    all_gather x2 -> x0, waiting for transfers between devices: 49.5 us -> none  [moe_layer(): lax.all_gather(arrived, 'dp', axis=0, tiled=True)]
    all_to_all x4 -> x0, starting transfers between devices: 29.2 us -> none  [the longest x2 20.2 us: moe_layer(): lax.all_to_all(partial_value.astype(jnp.bfloat16), 'expert', split_axis=0...]
    dot_general x6 -> x0, matrix products: 27.8 us -> none  [the longest x2 15 us: moe_layer(): jnp.einsum('secf,efd->secd', rows, e_out, preferred_element_type=jnp.floa...]
    reduce_sum x8 -> x0, other arithmetic: 10.5 us -> none  [the longest x2 5.63 us: summed_on_arrival(): return jnp.sum(blocks.astype(jnp.float32), axis=0)]
    unnamed x16 -> x5, local copies, waits for them, and re-layouts: 0.95 us -> 7.84 us
  transfers between devices with their start and end apart: 8 -> 0, of which waited for: 7 -> 0; matrix products, arithmetic and copies ran while one was open for 7% -> 0% of each run, Pallas kernels for 0% -> 0%
where the time goes in v1:
time: 149 us; the launch traced here: 147 us
  Pallas kernels  139 us (93%)
  local copies, waits for them, and re-layouts  7.84 us (5%)
    pallas_call x1, Pallas kernels, body(): pl.pallas_call(functools.partial(kernel, n_dp, n_ex), out_shape=jax.Shape...  139 us
    unnamed x5, local copies, waits for them, and re-layouts  7.84 us

profile of v1, /device:TPU:32, one launch (start us, length us, event | category | flops | bytes accessed | tf_op | source)
XLA Modules:
  0.0 146.8 jit_solution(8651434361497136727)
XLA Ops:
  0.0 1.4 copy.16.refs_1_
  1.4 1.4 copy.17.refs_2_
  2.8 1.7 %copy.18.refs_5_ = bf16[1024,32]{1,0:T(8,128)(2,1)} copy(bf16[1024,32]{0,1:T(8,128)(2,1)} %param.20) | data formatting | bytes 131072 | tf_op args[5]
  4.4 1.7 %copy.19.refs_6_ = bf16[1024,64]{1,0:T(8,128)(2,1)} copy(bf16[1024,64]{0,1:T(8,128)(2,1)} %param.21) | data formatting | bytes 262144 | tf_op args[6]
  6.2 139.0 %shard_map.145 = bf16[128,1024]{1,0:T(8,128)(2,1)} custom-call(bf16[128,1024]{1,0:T(8,128)(2,1)} %refs_0_.1, s32[128,1]{1,0:T(8,128)} %copy.16.refs_1_, s32[128,1]{1,0:T(8,128)} %copy.17.refs_2_, f32[1,1024]{1,0:T(1,128)} %bitcast.2, f32[1,1024]{1,0:T(1,128)} %bitcast.3, bf16[1024,32]{1,0:T(8,128)(2,1)} %copy.18.refs_5_, bf16[1024,64]{1,0:T(8,128)(2,1)} %copy.19.refs_6_, ...), custom_call_target="tpu_custom_call" | custom-call | tf_op jit(solution)/shard_map/pallas_call | solution.py:411
  145.1 1.7 %copy.21 = bf16[128,1024]{1,0:T(8,128)(2,1)} copy(bf16[128,1024]{1,0:T(8,128)(2,1)} %shard_map.145) | data formatting | bytes 524288

commit v2 on v1

--- a/solution.py
+++ b/solution.py
@@ -10,7 +10,7 @@
 MESH = pl.DeviceIdType.MESH
 BF = jnp.bfloat16
 F32 = jnp.float32
-PAD = 8
+LANES = 128
 
 
 def dot(a, b):
@@ -41,7 +41,8 @@
 
 
 class Ring:
-    def __init__(self, place, blocks, partial, kept, sums, landed, sems):
+    def __init__(self, name, place, blocks, partial, kept, sums, landed, sems):
+        self.name = name
         self.p = place
         self.g = blocks
         self.y1 = partial
@@ -87,15 +88,18 @@
 
     def arrive(self, u):
         for h in (0, 1):
-            self.gather_copy(u, h).wait_recv()
+            with jax.named_scope(f"w_{self.name}_gather{u}{h}"):
+                self.gather_copy(u, h).wait_recv()
             if u == 1:
                 self.start(self.gather_copy(3, h))
             self.start(self.core_copy(u, h))
 
     def compute(self, u, fn):
-        for h in (0, 1):
-            self.core_copy(u, h).wait_recv()
-        fn(u)
+        with jax.named_scope(f"w_{self.name}_core{u}"):
+            for h in (0, 1):
+                self.core_copy(u, h).wait_recv()
+        with jax.named_scope(f"c_{self.name}{u}"):
+            fn(u)
         for h in (0, 1):
             self.start(self.sum_copy(u, h))
 
@@ -103,7 +107,8 @@
         return self.copy(self.y1.at[u, h], self.z.at[u, h], 0, 8 + 2 * u + h, self.p.partner)
 
     def core_sum(self, u, h):
-        self.sum_copy(u, h).wait_recv()
+        with jax.named_scope(f"w_{self.name}_sum{u}{h}"):
+            self.sum_copy(u, h).wait_recv()
         return self.y0[u, h] + self.z[u, h].astype(F32)
 
     def scatter_copy(self, u, h):
@@ -124,15 +129,18 @@
     def scatter_last(self):
         for h in (0, 1):
             mine = self.core_sum(2, h)
-            self.scatter_copy(3, h).wait_recv()
+            with jax.named_scope(f"w_{self.name}_scatfar{h}"):
+                self.scatter_copy(3, h).wait_recv()
             self.s[2, h] = (mine + self.f[1, h].astype(F32)).astype(BF)
             self.start(self.scatter_copy(2, h))
 
     def total(self, h):
         mine = self.core_sum(0, h)
-        self.scatter_copy(1, h).wait_recv()
+        with jax.named_scope(f"w_{self.name}_scatnear{h}"):
+            self.scatter_copy(1, h).wait_recv()
         mine = mine + self.f[0, h].astype(F32)
-        self.scatter_copy(2, h).wait_recv()
+        with jax.named_scope(f"w_{self.name}_scatlast{h}"):
+            self.scatter_copy(2, h).wait_recv()
         return mine + self.f[2, h].astype(F32)
 
     def drain(self):
@@ -141,40 +149,46 @@
 
 
 class Exchange:
-    def __init__(self, place, out, into, send, recv, forward):
-        self.p, self.out, self.into, self.send, self.recv = place, out, into, send, recv
-        self.forward = forward
+    def __init__(self, place, rows, stage, refs, forward):
+        self.p, self.rows, self.forward = place, rows, forward
+        self.out, self.into, self.send, self.recv = refs
+        self.stage = stage.at[pl.ds(0, place.n_ex * rows)]
 
     def copy(self, o):
+        message = pl.ds(o * self.rows, self.rows)
         return pltpu.make_async_remote_copy(
-            src_ref=self.out.at[o],
-            dst_ref=self.into.at[o],
+            src_ref=self.out.at[message],
+            dst_ref=self.into.at[message],
             send_sem=self.send.at[o],
             recv_sem=self.recv.at[o],
             device_id=self.p.ahead(o) if self.forward else self.p.behind(o),
             device_id_type=MESH,
         )
 
-    def start(self):
+    def each(self, act):
         def one(o, carry):
-            self.copy(o).start()
+            act(self.copy(o))
             return carry
 
         lax.fori_loop(1, self.p.n_ex, one, 0)
 
+    def start(self, value):
+        for j in range(value.shape[1] // LANES):
+            self.stage[:, j, :] = value[:, j * LANES : (j + 1) * LANES]
+        tiles = self.stage[...].astype(BF)
+        self.out[...] = tiles
+        self.into[pl.ds(0, self.rows)] = tiles[: self.rows]
+        self.each(lambda copy: copy.start())
+
     def arrived(self):
-        def one(o, carry):
-            self.copy(o).wait_recv()
-            return carry
-
-        lax.fori_loop(1, self.p.n_ex, one, 0)
+        with jax.named_scope(f"w_a2a{int(self.forward)}"):
+            self.each(lambda copy: copy.wait_recv())
+        self.stage[...] = self.into[...].astype(F32)
+        columns = [self.stage[:, j, :] for j in range(self.into.shape[1])]
+        return jnp.concatenate(columns, axis=1).astype(BF)
 
     def drain(self):
-        def one(o, carry):
-            self.copy(o).wait_send()
-            return carry
-
-        lax.fori_loop(1, self.p.n_ex, one, 0)
+        self.each(lambda copy: copy.wait_send())
 
 
 def norm_rows(xf, gain):
@@ -188,31 +202,27 @@
 
 
 def routing(ids, place, experts, cap):
-    tok = ids.shape[0]
+    tok = ids.shape[1]
     per_dev = experts // place.n_ex
-    onehot = (ids == iota((tok, experts), 1)).astype(F32)
-    below = (iota((tok, tok), 1) < iota((tok, tok), 0)).astype(F32)
-    before = dot(below.astype(BF), onehot.astype(BF))
-    rank = jnp.sum(before * onehot, axis=-1, keepdims=True)
+    onehot = (iota((experts, tok), 0) == ids).astype(F32)
+    earlier = (iota((tok, tok), 0) < iota((tok, tok), 1)).astype(F32)
+    before = dot(onehot.astype(BF), earlier.astype(BF))
+    rank = jnp.sum(before * onehot, axis=0, keepdims=True)
     kept = rank < cap
     owner, inner = ids // per_dev, ids % per_dev
     offset = lax.rem(owner - place.e + place.n_ex, place.n_ex)
-    row = (offset * PAD + inner * cap).astype(F32) + rank
-    rows = place.n_ex * PAD
-    spot = jnp.where(kept & (iota((tok, rows), 1).astype(F32) == row), 1.0, 0.0)
+    row = ((offset * per_dev + inner) * cap).astype(F32) + rank
+    rows = place.n_ex * per_dev * cap
+    spot = jnp.where(kept & (iota((rows, tok), 0).astype(F32) == row), 1.0, 0.0)
     return onehot, kept, spot
 
 
-def packed_row(p, place, per_dev, cap):
-    source, inner = p // PAD, p % PAD
-    row = inner
-    which = jnp.zeros_like(p)
-    for k in range(1, per_dev):
-        which = which + (inner >= k * cap).astype(jnp.int32)
-    row = inner - which * cap
-    return jnp.where(
-        inner < per_dev * cap, which * (place.n_ex * cap) + source * cap + row, -1
-    )
+def by_expert(shape, dim, place, per_dev, cap):
+    message, packed = iota(shape, 1 - dim), iota(shape, dim)
+    source, inner = message // (per_dev * cap), message % (per_dev * cap)
+    which, rank = inner // cap, inner % cap
+    row = (which * place.n_ex + source) * cap + rank
+    return jnp.where(packed == row, 1.0, 0.0).astype(BF)
 
 
 def kernel(
@@ -242,27 +252,28 @@
     for i in (0, 1, 4, 5, 2, 3, 6, 7):
         loads[i].start()
 
-    kept_dense, kept_expert = scratch[:2]
-    per_layer = (len(scratch) - 2) // 2
+    kept_dense, kept_expert, stage = scratch[:3]
+    scratch = scratch[3:]
+    per_layer = len(scratch) // 2
     drains = []
     x = tokens[...].astype(F32)
     for layer in range(2):
-        s = scratch[2 + layer * per_layer : 2 + (layer + 1) * per_layer]
-        dense = Ring(place, s[0], s[1], kept_dense, s[2], s[3:5], s[5:9])
+        s = scratch[layer * per_layer : (layer + 1) * per_layer]
+        dense = Ring("d", place, s[0], s[1], kept_dense, s[2], s[3:5], s[5:9])
         s = s[9:]
         rows = s[0].shape[3]
         y0 = kept_expert.at[:, :, pl.ds(0, rows)]
-        expert = Ring(place, s[0], s[1], y0, s[2], s[3:5], s[5:9])
+        expert = Ring("e", place, s[0], s[1], y0, s[2], s[3:5], s[5:9])
         s = s[9:]
-        go = Exchange(place, s[0], s[1], s[2], s[3], True)
-        back = Exchange(place, s[4], s[5], s[6], s[7], False)
-        drains += [dense, expert, go, back]
-        ids = (route_a, route_b)[layer][...]
         router = (router_a, router_b)[layer][...]
-        experts = router.shape[1]
+        experts = router.shape[0]
         tok, width = tokens.shape
         per_dev = experts // n_ex
         cap = (5 * tok + 4 * experts - 1) // (4 * experts)
+        go = Exchange(place, per_dev * cap, stage, s[0:4], True)
+        back = Exchange(place, per_dev * cap, stage, s[4:8], False)
+        drains += [dense, expert, go, back]
+        ids = (route_a, route_b)[layer][...]
         d_in, d_out = local[4 * layer], local[4 * layer + 1]
         e_in, e_out = local[4 * layer + 2], local[4 * layer + 3]
         half = tok // 2
@@ -272,15 +283,16 @@
             dense.g[0, h, 0] = normed[h * half : (h + 1) * half]
         onehot, kept, spot = routing(ids, place, experts, cap)
         if layer == 0:
-            pl.semaphore_wait(barrier, n_ex - 1 + 3)
+            with jax.named_scope("w_barrier"):
+                pl.semaphore_wait(barrier, n_ex - 1 + 3)
         dense.gather_start()
-        messages = dot(spot.T.astype(BF), normed).astype(BF).reshape(n_ex, PAD, width)
-        go.out[...] = messages
-        go.into[0] = messages[0]
-        go.start()
-        logits = dot(normed, router)
-        picked = jnp.sum(logits * onehot, axis=-1, keepdims=True)
+        go.start(dot(spot.astype(BF), normed))
+        logits = lax.dot_general(
+            router, normed, (((1,), (1,)), ((), ())), preferred_element_type=F32
+        )
+        picked = jnp.sum(logits * onehot, axis=0, keepdims=True)
         gate = jax.nn.sigmoid(picked) * kept.astype(F32)
+        gate = jnp.broadcast_to(gate, (tok, tok)).T[:, :1]
 
         def dense_unit(u):
             y = ffn(dense.g[u].reshape(4 * half, width), d_in[...], d_out[...])
@@ -308,13 +320,10 @@
         dense.compute(1, dense_unit)
         dense.arrive(2)
 
-        go.arrived()
-        slots = n_ex * PAD
-        message = iota((2 * rows, slots), 1)
-        pack = packed_row(message, place, per_dev, cap) == iota((2 * rows, slots), 0)
-        block = dot(
-            jnp.where(pack, 1.0, 0.0).astype(BF), go.into[...].reshape(slots, width)
-        ).astype(BF)
+        block = go.arrived()
+        slots = (2 * rows, 2 * rows)
+        if per_dev > 1:
+            block = dot(by_expert(slots, 0, place, per_dev, cap), block).astype(BF)
         for h in (0, 1):
             expert.g[0, h, 0] = block[h * rows : (h + 1) * rows]
         expert.gather_start()
@@ -335,26 +344,21 @@
         dense.scatter_near()
         expert.scatter_last()
         dense.scatter_far()
-        block = jnp.concatenate([expert.total(h) for h in (0, 1)], axis=0).astype(BF)
-        message = iota((slots, 2 * rows), 0)
-        unpack = packed_row(message, place, per_dev, cap) == iota((slots, 2 * rows), 1)
-        messages = (
-            dot(jnp.where(unpack, 1.0, 0.0).astype(BF), block)
-            .astype(BF)
-            .reshape(n_ex, PAD, width)
-        )
-        back.out[...] = messages
-        back.into[0] = messages[0]
-        back.start()
+        block = jnp.concatenate([expert.total(h) for h in (0, 1)], axis=0)
+        if per_dev > 1:
+            block = dot(by_expert(slots, 1, place, per_dev, cap), block.astype(BF))
+        back.start(block)
         dense.scatter_last()
         summed = jnp.concatenate([dense.total(h) for h in (0, 1)], axis=0)
-        back.arrived()
-        found = dot(spot.astype(BF), back.into[...].reshape(slots, width))
+        found = lax.dot_general(
+            spot.astype(BF), back.arrived(), (((0,), (0,)), ((), ())), preferred_element_type=F32
+        )
         result = (x + summed + gate * found).astype(BF)
         x = result.astype(F32)
     out[...] = result
-    for thing in drains:
-        thing.drain()
+    with jax.named_scope("w_drain"):
+        for thing in drains:
+            thing.drain()
 
 
 def ring_scratch(rows, width):
@@ -372,8 +376,8 @@
     ]
 
 
-def exchange_scratch(n_ex, width):
-    one = pltpu.VMEM((n_ex, PAD, width), BF)
+def exchange_scratch(n_ex, slots, width):
+    one = pltpu.VMEM((slots, width // LANES, LANES), BF)
     sem = pltpu.SemaphoreType.DMA((n_ex,))
     return [one, one, sem, sem]
 
@@ -403,9 +407,10 @@
         rows = experts * cap // 2
         per_half.append(rows)
         layers += ring_scratch(tok // 2, width) + ring_scratch(rows, width)
-        layers += exchange_scratch(n_ex, width) * 2
+        layers += exchange_scratch(n_ex, 2 * rows, width) * 2
     scratch.append(pltpu.VMEM((4, 2, tok // 2, width), F32))
     scratch.append(pltpu.VMEM((4, 2, max(per_half), width), F32))
+    scratch.append(pltpu.VMEM((2 * max(per_half), width // LANES, LANES), F32))
     scratch += layers
     vmem = pl.BlockSpec(memory_space=pltpu.VMEM)
     return pl.pallas_call(
@@ -419,12 +424,12 @@
         ),
     )(
         tokens,
-        route_a,
-        route_b,
+        route_a.reshape(1, tok),
+        route_b.reshape(1, tok),
         gain_a.reshape(1, width),
         gain_b.reshape(1, width),
-        router_a,
-        router_b,
+        router_a.T,
+        router_b.T,
         *weights,
     )
 

time: 149 us -> 131 us (0.88); the launches traced: 147 us -> 131 us
  Pallas kernels: 139 us -> 129 us
  local copies, waits for them, and re-layouts: 7.84 us -> 1.67 us
    pallas_call x1, Pallas kernels: 139 us -> 129 us  [body(): pl.pallas_call(functools.partial(kernel, n_dp, n_ex), out_shape=jax.Shape...]
    unnamed x5 -> x1, local copies, waits for them, and re-layouts: 7.84 us -> 1.67 us
where the time goes in v2:
time: 131 us
  Pallas kernels  129 us (98%)
  local copies, waits for them, and re-layouts  1.67 us (1%)
    pallas_call x1, Pallas kernels, body(): pl.pallas_call(functools.partial(kernel, n_dp, n_ex), out_shape=jax.Shape...  129 us

profile of v2, /device:TPU:32, one launch (start us, length us, event | category | flops | bytes accessed | tf_op | source)
XLA Modules:
  0.0 130.6 jit_solution(11054774118891942178)
XLA Ops:
  0.0 128.9 %shard_map.145 = bf16[128,1024]{1,0:T(8,128)(2,1)} custom-call(bf16[128,1024]{1,0:T(8,128)(2,1)} %refs_0_.1, s32[1,128]{1,0:T(1,128)} %bitcast.10, s32[1,128]{1,0:T(1,128)} %bitcast.11, f32[1,1024]{1,0:T(1,128)} %bitcast.8, f32[1,1024]{1,0:T(1,128)} %bitcast.9, bf16[32,1024]{1,0:T(8,128)(2,1)} %bitcast.7, bf16[64,1024]{1,0:T(8,128)(2,1)} %bitcast.6, ...), custom_call_target="tpu_custom_call" | custom-call | tf_op jit(solution)/shard_map/pallas_call | solution.py:416
  128.9 1.7 %copy.17 = bf16[128,1024]{1,0:T(8,128)(2,1)} copy(bf16[128,1024]{1,0:T(8,128)(2,1)} %shard_map.145) | data formatting | bytes 524288
